TPU v7x, 256 devices: a whole 4x4x8 slice. The times are simulated.
256 devices in a mesh: outer: 16 (over z_lo, x), inner: 16 (over y, z_hi, core).
Axes of the slice: x: 4, y: 4, z: 8 (z_hi: 2, z_lo: 4; z = z_hi * 4 + z_lo), core: 2. Of those that a mesh axis runs over, the one named last changes fastest.
Arguments:
- queries: bfloat16 [8192, 2, 4096], P('outer', None, 'inner'), may hold values from -52 to 52
- keys: bfloat16 [8192, 2, 4096], P('outer', None, 'inner'), may hold values from -6 to 6
- values: bfloat16 [8192, 2, 4096], P('outer', None, 'inner'), may hold values from -6 to 6
Outputs:
- attended: bfloat16 [8192, 2, 4096], P(('outer', 'inner'))
All inputs are finite; a program needn't handle non-finite values.
Results may differ from a plain program's by a relative error of at most 0.004.
Values may be sent and summed in bfloat16 or wider, within the bound.
A program may use at most 128 MiB of HBM per device.

v0:
```python
from functools import partial
import math
import jax
import jax.numpy as jnp
from jax import lax
from jax.sharding import PartitionSpec as P

HEAD_DIM = 128


def attend_keys(running, key_block, value_block, query_heads, head_count):
    peak_rows, totals, numerator = running
    key_count = key_block.shape[0]
    key_heads = key_block.reshape(key_count, head_count, HEAD_DIM)
    value_heads = value_block.reshape(key_count, head_count, HEAD_DIM)
    scores = jnp.einsum(
        "qhd,khd->qhk", query_heads, key_heads, preferred_element_type=jnp.float32
    ) * (1.0 / math.sqrt(HEAD_DIM))
    new_peaks = jnp.maximum(peak_rows, jnp.max(scores, axis=2))
    shrink = jnp.exp(peak_rows - new_peaks)
    weights = jnp.exp(scores - new_peaks[..., None])
    totals = totals * shrink + jnp.sum(weights, axis=2)
    numerator = numerator * shrink[..., None] + jnp.einsum(
        "qhk,khd->qhd",
        weights.astype(jnp.bfloat16),
        value_heads,
        preferred_element_type=jnp.float32,
    )
    return (new_peaks, totals, numerator)


def attend_piece(running, pieces, start_row, query_part, head_count):
    key_rows, value_rows = pieces
    row_count = query_part.shape[0]
    query_heads = query_part.reshape(row_count, head_count, HEAD_DIM)
    block_count = key_rows.shape[0] // row_count
    key_blocks = key_rows.reshape(block_count, row_count, key_rows.shape[1])
    value_blocks = value_rows.reshape(block_count, row_count, value_rows.shape[1])

    def one_block(state, blocks):
        return (attend_keys(state, blocks[0], blocks[1], query_heads, head_count), None)

    running, unused = lax.scan(one_block, running, (key_blocks, value_blocks))
    return running


def start_state(row_count, head_count):
    peak_rows = jnp.full((row_count, head_count), -1e30, jnp.float32)
    totals = jnp.zeros((row_count, head_count), jnp.float32)
    numerator = jnp.zeros((row_count, head_count, HEAD_DIM), jnp.float32)
    return (peak_rows, totals, numerator)


def finish_state(running):
    peak_rows, totals, numerator = running
    averaged = numerator / totals[..., None]
    return averaged.reshape(numerator.shape[0], -1).astype(jnp.bfloat16)


def flatten(array):
    return array.reshape(array.shape[0], array.shape[1] * array.shape[2])


def per_device(queries, keys, values):
    tok_rows, networks, local_cols = queries.shape
    flat_queries, flat_keys, flat_values = (flatten(queries), flatten(keys), flatten(values))
    head_count = networks * local_cols // HEAD_DIM
    folder = partial(attend_piece, query_part=flat_queries, head_count=head_count)
    running = folder(
        start_state(tok_rows, head_count),
        (
            lax.all_gather(flat_keys, "outer", axis=0, tiled=True),
            lax.all_gather(flat_values, "outer", axis=0, tiled=True),
        ),
        jnp.int32(0),
    )
    local_out = finish_state(running).reshape(tok_rows, networks, local_cols)
    attended = lax.all_to_all(local_out, "inner", split_axis=0, concat_axis=2, tiled=True)
    return attended


def solution(mesh):
    return jax.shard_map(
        per_device,
        mesh=mesh,
        in_specs=(P("outer", None, "inner"), P("outer", None, "inner"), P("outer", None, "inner")),
        out_specs=P(("outer", "inner"), None, None),
        check_vma=False,
    )
```

profile of v0, /device:TPU:32, one launch (start us, length us, event | category | flops | bytes accessed | tf_op | source)
XLA Modules:
  0.0 320.9 jit_solution(2837683536750189921)
XLA Ops:
  6.5 1.9 copy.35
  8.5 1.9 copy.36
  10.5 1.3 copy.21
  12.1 99.0 %all-gather.3.cloned.1.call-done = bf16[8192,512]{1,0:T(8,128)(2,1)} async-done(((bf16[512,512]{1,0:T(8,128)(2,1)}), bf16[8192,512]{1,0:T(8,128)(2,1)}) %all-gather.3.cloned.1.call-update) | async-done | bytes 8388624 | tf_op jit(solution)/shard_map/all_gather | solution.py:72
  111.1 101.0 %all-gather.5.cloned.1.call-done = bf16[8192,512]{1,0:T(8,128)(2,1)} async-done(((bf16[512,512]{1,0:T(8,128)(2,1)}), bf16[8192,512]{1,0:T(8,128)(2,1)}) %all-gather.5.cloned.1.call-update) | async-done | bytes 8388624 | tf_op jit(solution)/shard_map/all_gather | solution.py:73
  212.0 70.4 %while.15 = (s32[]{:T(128)}, f32[512,4]{0,1:T(4,128)S(1)}, f32[512,4]{0,1:T(4,128)S(1)}, f32[512,4,128]{0,2,1:T(8,128)S(1)}, bf16[16,512,512]{2,1,0:T(8,128)(2,1...) while((s32[]{:T(128)}, f32[512,4]{0,1:T(4,128)S(1)}, ...), condition=%wide.region_3.4_spmd.clone, body=%wide.region_0.3_spmd.clone.sunk | while | flops 546056192 | bytes 20578420 | solution.py:43
  212.0 1.3 constant_dynamic-slice_fusion.3
  215.2 1.1 fusion.31
  216.4 1.3 constant_dynamic-slice_fusion.3
  219.6 1.1 fusion.31
  220.8 1.3 constant_dynamic-slice_fusion.3
  224.1 1.1 fusion.31
  225.2 1.3 constant_dynamic-slice_fusion.3
  228.5 1.1 fusion.31
  229.6 1.3 constant_dynamic-slice_fusion.3
  232.9 1.1 fusion.31
  234.0 1.3 constant_dynamic-slice_fusion.3
  237.3 1.1 fusion.31
  238.4 1.3 constant_dynamic-slice_fusion.3
  241.7 1.1 fusion.31
  242.8 1.3 constant_dynamic-slice_fusion.3
  247.3 1.3 constant_dynamic-slice_fusion.3
  250.5 1.1 fusion.31
  251.7 1.3 constant_dynamic-slice_fusion.3
  254.9 1.1 fusion.31
  256.1 1.3 constant_dynamic-slice_fusion.3
  260.5 1.3 constant_dynamic-slice_fusion.3
  264.9 1.3 constant_dynamic-slice_fusion.3
  269.3 1.3 constant_dynamic-slice_fusion.3
  273.7 1.3 constant_dynamic-slice_fusion.3
  278.1 1.3 constant_dynamic-slice_fusion.3
  283.1 29.7 %all_to_all.18 = bf16[512,2,256]{2,1,0:T(2,128)(2,1)S(1)} all-to-all(bf16[512,2,256]{2,1,0:T(2,128)(2,1)S(1)} %copy.25), channel_id=1, replica_groups=mesh['outer'=16,'inner'=16] {'inner'}, dimensions={0} | all-to-all | bytes 1048576 | tf_op jit(solution)/shard_map/all_to_all | solution.py:78
  (132 shorter events, 41.2 us)
Async XLA Ops:
  6.5 104.5 %all-gather.3.cloned.1.call-start = ((), (), s32[]{:S(2)}) async-start(), calls=%async_computation.1 | async-start | bytes 8912896 | tf_op jit(solution)/shard_map/all_gather | solution.py:72
  8.5 203.5 %all-gather.5.cloned.1.call-start = ((), (), s32[]{:S(2)}) async-start(), calls=%async_computation.2 | async-start | bytes 8912896 | tf_op jit(solution)/shard_map/all_gather | solution.py:73
Sparse Core Ops, SparseCore 0:
  9.1 101.9 all-gather.2
  112.9 99.1 all-gather.4
where the time goes:
time: 322 us; the launch traced here: 321 us
  waiting for transfers between devices  200 us (62%)
  local copies, waits for them, and re-layouts  34.4 us (11%)
  matrix products  30.6 us (10%)
  blocking collectives  29.7 us (9%)
  between operations  13.5 us (4%)
  other arithmetic  11.9 us (4%)
    all_gather x1, waiting for transfers between devices, per_device(): lax.all_gather(flat_values, 'outer', axis=0, tiled=True)  101 us
    all_gather x1, waiting for transfers between devices, per_device(): lax.all_gather(flat_keys, 'outer', axis=0, tiled=True)  99 us
    all_to_all x1, blocking collectives, per_device(): lax.all_to_all(local_out, 'inner', split_axis=0, concat_axis=2, tiled=True)  29.7 us
    dynamic_slice x48, local copies, waits for them, and re-layouts, attend_piece(): running, unused = lax.scan(one_block, running, (key_blocks, value_blocks))  27.2 us
    dot_general x16, matrix products, attend_keys(): jnp.einsum('qhk,khd->qhd', weights.astype(jnp.bfloat16), value_heads, pre...  18.3 us
    dot_general x16, matrix products, attend_keys(): jnp.einsum('qhd,khd->qhk', query_heads, key_heads, preferred_element_type...  12.4 us
    reduce_sum x16, other arithmetic, attend_keys(): totals = totals * shrink + jnp.sum(weights, axis=2)  11.3 us
  transfers between devices with their start and end apart: 2, of which 2 were waited for; matrix products, arithmetic and copies ran while one was open for 1% of the time, Pallas kernels for 0%

commit v1 on v0

--- a/solution.py
+++ b/solution.py
@@ -70,7 +70,10 @@
         start_state(tok_rows, head_count),
         (
             lax.all_gather(flat_keys, "outer", axis=0, tiled=True),
-            lax.all_gather(flat_values, "outer", axis=0, tiled=True),
+            jnp.concatenate(
+                lax.all_to_all(jnp.stack([flat_values] * lax.axis_size("outer")), "outer", 0, 0),
+                axis=0,
+            ),
         ),
         jnp.int32(0),
     )

time: 322 us -> 479 us (1.49); the launches traced: 321 us -> 470 us
  waiting for transfers between devices: 200 us -> 267 us
  other arithmetic: 11.9 us -> 49.4 us
  matrix products: 30.6 us -> 61.5 us
  local copies, waits for them, and re-layouts: 34.4 us -> 47.1 us
  starting transfers between devices: 0.04 us -> 8.65 us
  blocking collectives: 29.7 us -> 22.3 us
    all_to_all x0 -> x1, waiting for transfers between devices: none -> 267 us  [per_device(): lax.all_to_all(jnp.stack([flat_values] * lax.axis_size('outer')), 'outer'...]
    all_gather x1 -> x0, waiting for transfers between devices: 101 us -> none  [per_device(): lax.all_gather(flat_values, 'outer', axis=0, tiled=True)]
    all_gather x1, waiting for transfers between devices: 99 us -> 0.01 us  [per_device(): lax.all_gather(flat_keys, 'outer', axis=0, tiled=True)]
    reduce_sum x16, other arithmetic: 11.3 us -> 48.9 us  [attend_keys(): totals = totals * shrink + jnp.sum(weights, axis=2)]
    dot_general x16, matrix products: 12.4 us -> 43.2 us  [attend_keys(): jnp.einsum('qhd,khd->qhk', query_heads, key_heads, preferred_element_type...]
    dynamic_slice x48, local copies, waits for them, and re-layouts: 27.2 us -> 38 us  [attend_piece(): running, unused = lax.scan(one_block, running, (key_blocks, value_blocks))]
    all_to_all x0 -> x1, starting transfers between devices: none -> 8.61 us  [per_device(): lax.all_to_all(jnp.stack([flat_values] * lax.axis_size('outer')), 'outer'...]
    all_to_all x1, blocking collectives: 29.7 us -> 22.3 us  [per_device(): lax.all_to_all(local_out, 'inner', split_axis=0, concat_axis=2, tiled=True)]
  transfers between devices with their start and end apart: 2 -> 2, of which waited for: 2 -> 1; matrix products, arithmetic and copies ran while one was open for 1% -> 0% of each run, Pallas kernels for 0% -> 0%
where the time goes in v1:
time: 479 us; the launch traced here: 470 us
  waiting for transfers between devices  267 us (56%)
  matrix products  61.5 us (13%)
  other arithmetic  49.4 us (10%)
  local copies, waits for them, and re-layouts  47.1 us (10%)
  blocking collectives  22.3 us (5%)
  between operations  13.5 us (3%)
  starting transfers between devices  8.65 us (2%)
    all_to_all x1, waiting for transfers between devices, per_device(): lax.all_to_all(jnp.stack([flat_values] * lax.axis_size('outer')), 'outer'...  267 us
    reduce_sum x16, other arithmetic, attend_keys(): totals = totals * shrink + jnp.sum(weights, axis=2)  48.9 us
    dot_general x16, matrix products, attend_keys(): jnp.einsum('qhd,khd->qhk', query_heads, key_heads, preferred_element_type...  43.2 us
    dynamic_slice x48, local copies, waits for them, and re-layouts, attend_piece(): running, unused = lax.scan(one_block, running, (key_blocks, value_blocks))  38 us
    all_to_all x1, blocking collectives, per_device(): lax.all_to_all(local_out, 'inner', split_axis=0, concat_axis=2, tiled=True)  22.3 us
    dot_general x16, matrix products, attend_keys(): jnp.einsum('qhk,khd->qhd', weights.astype(jnp.bfloat16), value_heads, pre...  18.3 us
  transfers between devices with their start and end apart: 2, of which 1 were waited for; matrix products, arithmetic and copies ran while one was open for 0% of the time, Pallas kernels for 0%

profile of v1, /device:TPU:32, one launch (start us, length us, event | category | flops | bytes accessed | tf_op | source)
XLA Modules:
  0.0 470.1 jit_solution(4714705554312195685)
XLA Ops:
  7.8 4.0 stack.3
  11.9 8.6 %all-to-all-start = ((bf16[16,512,512]{1,2,0:T(8,128)(2,1)}), bf16[16,512,512]{1,2,0:T(8,128)(2,1)}, u32[]{:S(2)}, u32[]{:S(2)}) async-start(bf16[16,512,512]{1,2,0:T(8,128)(2,1)} %stack.3), calls=%async_computation | async-start | bytes 16777216 | tf_op jit(solution)/shard_map/all_to_all | solution.py:74
  22.5 266.6 %all-to-all-done = bf16[16,512,512]{1,2,0:T(8,128)(2,1)} async-done(((bf16[16,512,512]{1,2,0:T(8,128)(2,1)}), bf16[16,512,512]{1,2,0:T(8,128)(2,1)}, u32[]{:S(2)}, u32[]{:S(2)}) %all-to-all-start) | async-done | bytes 8388640 | tf_op jit(solution)/shard_map/all_to_all | solution.py:74
  289.2 149.8 %while.15 = (s32[]{:T(128)}, f32[512,4]{0,1:T(4,128)S(1)}, f32[512,4]{0,1:T(4,128)S(1)}, f32[512,4,128]{0,2,1:T(8,128)S(1)}, bf16[16,512,512]{2,1,0:T(8,128)(2,1...) while((s32[]{:T(128)}, f32[512,4]{0,1:T(4,128)S(1)}, ...), condition=%wide.region_3.4_spmd.clone, body=%wide.region_0.3_spmd.clone.sunk | while | flops 546056192 | bytes 36307084 | solution.py:43
  290.5 2.7 bitcast_reduce_fusion.2
  293.2 3.1 fusion.29
  299.8 2.7 bitcast_reduce_fusion.2
  302.5 3.1 fusion.29
  309.2 2.7 bitcast_reduce_fusion.2
  311.9 3.1 fusion.29
  318.6 2.7 bitcast_reduce_fusion.2
  321.3 3.1 fusion.29
  327.9 2.7 bitcast_reduce_fusion.2
  330.6 3.1 fusion.29
  337.3 2.7 bitcast_reduce_fusion.2
  340.0 3.1 fusion.29
  349.4 3.1 fusion.29
  356.0 2.7 bitcast_reduce_fusion.2
  358.7 3.1 fusion.29
  368.1 3.1 fusion.29
  374.7 2.7 bitcast_reduce_fusion.2
  377.5 3.1 fusion.29
  386.8 3.1 fusion.29
  393.5 2.7 bitcast_reduce_fusion.2
  396.2 3.1 fusion.29
  405.6 3.1 fusion.29
  412.2 2.7 bitcast_reduce_fusion.2
  414.9 3.1 fusion.29
  424.3 3.1 fusion.29
  430.9 2.7 bitcast_reduce_fusion.2
  433.6 3.1 fusion.29
  439.6 22.3 %all_to_all.23 = bf16[512,2,256]{2,1,0:T(2,128)(2,1)S(1)} all-to-all(bf16[512,2,256]{2,1,0:T(2,128)(2,1)S(1)} %copy.26), channel_id=1, replica_groups=mesh['outer'=16,'inner'=16] {'inner'}, dimensions={0} | all-to-all | bytes 1048576 | tf_op jit(solution)/shard_map/all_to_all | solution.py:81
  (168 shorter events, 75.4 us)
Async XLA Ops:
  11.9 8.7 %copy-start.1 = (bf16[512,2,256]{2,1,0:T(2,128)(2,1)S(1)}, bf16[512,2,256]{2,1,0:T(2,128)(2,1)}, u32[]{:S(2)}) copy-start(bf16[512,2,256]{2,1,0:T(2,128)(2,1)} %param.6) | copy-start | bytes 1572868
  11.9 9.6 %copy-start.2 = (bf16[512,2,256]{2,1,0:T(2,128)(2,1)S(1)}, bf16[512,2,256]{2,1,0:T(2,128)(2,1)}, u32[]{:S(2)}) copy-start(bf16[512,2,256]{2,1,0:T(2,128)(2,1)} %param.5) | copy-start | bytes 1572868
  11.9 277.3 %all-to-all-start = ((bf16[16,512,512]{1,2,0:T(8,128)(2,1)}), bf16[16,512,512]{1,2,0:T(8,128)(2,1)}, u32[]{:S(2)}, u32[]{:S(2)}) async-start(bf16[16,512,512]{1,2,0:T(8,128)(2,1)} %stack.3), calls=%async_computation | async-start | bytes 16777216 | tf_op jit(solution)/shard_map/all_to_all | solution.py:74
  20.5 268.7 %all-gather.2.cloned.1.call-start = ((), (), s32[]{:S(2)}) async-start(), calls=%async_computation.2 | async-start | bytes 8912896 | tf_op jit(solution)/shard_map/all_gather | solution.py:72
  293.2 4.2 copy-start
  302.5 4.2 copy-start
  311.9 4.2 copy-start
  321.3 4.2 copy-start
  330.6 4.2 copy-start
  340.0 4.2 copy-start
  349.4 4.2 copy-start
  358.7 4.2 copy-start
  368.1 4.2 copy-start
  377.5 4.2 copy-start
  386.8 4.2 copy-start
  396.2 4.2 copy-start
  405.5 4.2 copy-start
  414.9 4.2 copy-start
  424.3 4.2 copy-start
  433.6 4.2 copy-start
Sparse Core Ops, SparseCore 0:
  23.1 245.1 all-gather.1

commit v2 on v0

--- a/solution.py
+++ b/solution.py
@@ -75,7 +75,12 @@
         jnp.int32(0),
     )
     local_out = finish_state(running).reshape(tok_rows, networks, local_cols)
-    attended = lax.all_to_all(local_out, "inner", split_axis=0, concat_axis=2, tiled=True)
+    attended = jnp.concatenate(
+        lax.all_to_all(
+            jnp.stack(jnp.split(local_out, lax.axis_size("inner"), axis=0)), "inner", 0, 0
+        ),
+        axis=2,
+    )
     return attended
 
 

time: 322 us -> 324 us (level)
  no operation moved by 1% of the time
where the time goes in v2:
time: 324 us; the launch traced here: 323 us
  waiting for transfers between devices  200 us (62%)
  local copies, waits for them, and re-layouts  36.8 us (11%)
  matrix products  30.6 us (9%)
  blocking collectives  29.7 us (9%)
  between operations  13.6 us (4%)
  other arithmetic  11.9 us (4%)
    all_gather x1, waiting for transfers between devices, per_device(): lax.all_gather(flat_values, 'outer', axis=0, tiled=True)  101 us
    all_gather x1, waiting for transfers between devices, per_device(): lax.all_gather(flat_keys, 'outer', axis=0, tiled=True)  99 us
    all_to_all x1, blocking collectives, per_device(): lax.all_to_all(jnp.stack(jnp.split(local_out, lax.axis_size('inner'), axi...  29.7 us
    dynamic_slice x48, local copies, waits for them, and re-layouts, attend_piece(): running, unused = lax.scan(one_block, running, (key_blocks, value_blocks))  27.2 us
    dot_general x16, matrix products, attend_keys(): jnp.einsum('qhk,khd->qhd', weights.astype(jnp.bfloat16), value_heads, pre...  18.3 us
    dot_general x16, matrix products, attend_keys(): jnp.einsum('qhd,khd->qhk', query_heads, key_heads, preferred_element_type...  12.4 us
    reduce_sum x16, other arithmetic, attend_keys(): totals = totals * shrink + jnp.sum(weights, axis=2)  11.3 us
  transfers between devices with their start and end apart: 2, of which 2 were waited for; matrix products, arithmetic and copies ran while one was open for 1% of the time, Pallas kernels for 0%

profile of v2, /device:TPU:32, one launch (start us, length us, event | category | flops | bytes accessed | tf_op | source)
XLA Modules:
  0.0 323.5 jit_solution(6103479896864559688)
XLA Ops:
  6.5 1.9 copy.133
  8.5 1.9 copy.134
  10.5 1.3 copy.88
  12.1 99.0 %all-gather.3.cloned.1.call-done = bf16[8192,512]{1,0:T(8,128)(2,1)} async-done(((bf16[512,512]{1,0:T(8,128)(2,1)}), bf16[8192,512]{1,0:T(8,128)(2,1)}) %all-gather.3.cloned.1.call-update) | async-done | bytes 8388624 | tf_op jit(solution)/shard_map/all_gather | solution.py:72
  111.1 101.0 %all-gather.5.cloned.1.call-done = bf16[8192,512]{1,0:T(8,128)(2,1)} async-done(((bf16[512,512]{1,0:T(8,128)(2,1)}), bf16[8192,512]{1,0:T(8,128)(2,1)}) %all-gather.5.cloned.1.call-update) | async-done | bytes 8388624 | tf_op jit(solution)/shard_map/all_gather | solution.py:73
  212.0 70.4 %while.15 = (s32[]{:T(128)}, f32[512,4]{0,1:T(4,128)S(1)}, f32[512,4]{0,1:T(4,128)S(1)}, f32[512,4,128]{0,2,1:T(8,128)S(1)}, bf16[16,512,512]{2,1,0:T(8,128)(2,1...) while((s32[]{:T(128)}, f32[512,4]{0,1:T(4,128)S(1)}, ...), condition=%wide.region_3.4_spmd.clone, body=%wide.region_0.3_spmd.clone.sunk | while | flops 546056192 | bytes 20578420 | solution.py:43
  212.0 1.3 constant_dynamic-slice_fusion.3
  215.2 1.1 fusion.32
  216.4 1.3 constant_dynamic-slice_fusion.3
  219.6 1.1 fusion.32
  220.8 1.3 constant_dynamic-slice_fusion.3
  224.1 1.1 fusion.32
  225.2 1.3 constant_dynamic-slice_fusion.3
  228.5 1.1 fusion.32
  229.6 1.3 constant_dynamic-slice_fusion.3
  232.9 1.1 fusion.32
  234.0 1.3 constant_dynamic-slice_fusion.3
  237.3 1.1 fusion.32
  238.4 1.3 constant_dynamic-slice_fusion.3
  241.7 1.1 fusion.32
  242.8 1.3 constant_dynamic-slice_fusion.3
  247.3 1.3 constant_dynamic-slice_fusion.3
  250.5 1.1 fusion.32
  251.7 1.3 constant_dynamic-slice_fusion.3
  256.1 1.3 constant_dynamic-slice_fusion.3
  260.5 1.3 constant_dynamic-slice_fusion.3
  264.9 1.3 constant_dynamic-slice_fusion.3
  269.3 1.3 constant_dynamic-slice_fusion.3
  273.7 1.3 constant_dynamic-slice_fusion.3
  278.1 1.3 constant_dynamic-slice_fusion.3
  285.6 29.7 %all_to_all.5 = bf16[16,32,2,256]{3,2,1,0:T(2,128)(2,1)S(1)} all-to-all(bf16[16,32,2,256]{3,2,1,0:T(2,128)(2,1)S(1)} %constant_dynamic-update-slice_fusion), channel_id=1, replica_groups=mesh['outer'=16,'inner'=16] {'inner'}, dimensions={0} | all-to-all | bytes 1048576 | tf_op jit(solution)/shard_map/all_to_all | solution.py:79
  315.3 1.4 copy.132
  (162 shorter events, 43.4 us)
Async XLA Ops:
  6.5 104.5 %all-gather.3.cloned.1.call-start = ((), (), s32[]{:S(2)}) async-start(), calls=%async_computation.1 | async-start | bytes 8912896 | tf_op jit(solution)/shard_map/all_gather | solution.py:72
  8.5 203.5 %all-gather.5.cloned.1.call-start = ((), (), s32[]{:S(2)}) async-start(), calls=%async_computation.2 | async-start | bytes 8912896 | tf_op jit(solution)/shard_map/all_gather | solution.py:73
Sparse Core Ops, SparseCore 0:
  9.1 101.9 all-gather.2
  112.9 99.1 all-gather.4
